TPU v7x, 1024 devices: a whole 4x4x32 slice. The times are simulated.
1024 devices in a mesh: segment: 2 (over y_hi), win: 32 (over z), seq: 16 (over y_lo, x, core).
Axes of the slice: x: 4, y: 4 (y_hi: 2, y_lo: 2; y = y_hi * 2 + y_lo), z: 32, core: 2. Of those that a mesh axis runs over, the one named last changes fastest.
Arguments:
- latents: bfloat16 [2, 32, 1024, 1536], P('segment', 'seq', 'win'), may hold values from -6 to 6
- timesteps: int32 [2], P('segment'), may hold values from 0 to 31, as said below
- offsets: int32 [2, 2], P('segment'), may hold values from 1 to 31
- qkv_weight: bfloat16 [2, 1536, 16, 288], P('segment', None, 'seq'), may hold values from -0.15309311 to 0.15309311
- logit_scale: float32 [2, 16], P('segment', 'seq'), may hold values from 4 to 256
- out_weight: bfloat16 [2, 1536, 1536], P('segment'), may hold values from -0.15625 to 0.15625
- mod_shift: float32 [2, 32, 1536], P('segment'), may hold values from -3 to 3
- mod_scale: float32 [2, 32, 1536], P('segment'), may hold values from 0.5 to 1.5
- mod_gate: float32 [2, 32, 1536], P('segment'), may hold values from 1 to 3
Outputs:
- handed: bfloat16 [2, 32, 1024, 1536], P('segment', 'seq', 'win')
Inputs may be any that keep to these rules, and one draw needn't show every extreme that they name: `timesteps`: the sections' noise levels differ from one another.
All inputs are finite; a program needn't handle non-finite values.
Results may differ from a plain program's by a relative error of at most 0.015.
Values may be sent and summed in bfloat16 or wider, within the bound.
A program may use at most 32 MiB of HBM per device.

v0:
```python
import jax
import jax.numpy as jnp
from jax import lax
from jax.sharding import PartitionSpec as P

eps_norm = 1e-06
masked = -1e30


def passed_along(block, axis, distance):
    devices = range(lax.axis_size(axis))
    route = [((i - distance) % len(devices), i) for i in devices]
    return lax.ppermute(block, axis, route)


def unit_split(mixture, size):
    queries = mixture[..., :size]
    key_part = mixture[..., size : 2 * size]
    values = mixture[..., 2 * size :]
    queries = queries * lax.rsqrt(jnp.sum(queries * queries, -1, keepdims=True) + eps_norm)
    key_part = key_part * lax.rsqrt(jnp.sum(key_part * key_part, -1, keepdims=True) + eps_norm)
    return jnp.concatenate([queries, key_part, values], -1).astype(jnp.bfloat16)


def table_row(table, noise_level):
    onehot = (lax.iota(jnp.int32, table.shape[0]) == noise_level).astype(jnp.float32)
    return jnp.dot(
        onehot, table, precision=lax.Precision.HIGHEST, preferred_element_type=jnp.float32
    )


def shards(
    latents, timesteps, offsets, qkv_weight, logit_scale, out_weight, mod_shift, mod_scale, mod_gate
):
    local_tile = latents[0]
    row_count, col_count, model_width = local_tile.shape
    heads_here = qkv_weight.shape[2]
    head_size = qkv_weight.shape[3] // 3
    seq_count = lax.axis_size("seq")
    inner_here = heads_here * head_size
    noise_level = timesteps[0]
    lat_offset = offsets[0, 0]
    lon_offset = offsets[0, 1]
    shift_row = table_row(mod_shift[0], noise_level)
    scale_row = table_row(mod_scale[0], noise_level)
    gate_row = table_row(mod_gate[0], noise_level)
    neighbour = passed_along(local_tile, "win", -1)
    joined = jnp.concatenate([local_tile, neighbour], axis=1)
    shifted = lax.dynamic_slice_in_dim(joined, lon_offset, col_count, 1)
    residual = shifted.astype(jnp.float32)
    average = jnp.mean(residual, -1, keepdims=True)
    centred = residual - average
    variance = jnp.mean(centred * centred, -1, keepdims=True)
    normed = (centred * lax.rsqrt(variance + eps_norm) * scale_row + shift_row).astype(jnp.bfloat16)
    weights = qkv_weight[0].reshape(model_width, heads_here * 3 * head_size)
    shard_rows = lax.all_gather(normed, "seq", axis=0, tiled=True)
    mixture = jnp.dot(
        shard_rows.reshape(-1, model_width), weights, preferred_element_type=jnp.float32
    )
    mixture = mixture.reshape(shard_rows.shape[0], col_count, heads_here, 3 * head_size)
    gathered = unit_split(mixture, head_size)
    window = jnp.roll(gathered, -lat_offset, axis=0)
    side = window.shape[0]
    token_total = side * col_count
    tokens = window.reshape(token_total, heads_here, 3 * head_size)
    query_unit = tokens[..., :head_size]
    key_unit = tokens[..., head_size : 2 * head_size]
    value_rows = tokens[..., 2 * head_size :]
    token_group = lax.iota(jnp.int32, token_total) // col_count >= side - lat_offset
    scales = logit_scale[0]
    block_rows = min(512, token_total)
    block_count = token_total // block_rows

    def attend(block_index):
        first = block_index * block_rows
        query_block = lax.dynamic_slice_in_dim(query_unit, first, block_rows, 0)
        group_block = lax.dynamic_slice_in_dim(token_group, first, block_rows, 0)
        scores = (
            jnp.einsum("qhd,khd->hqk", query_block, key_unit, preferred_element_type=jnp.float32)
            * scales[:, None, None]
        )
        allowed = group_block[:, None] == token_group[None, :]
        scores = jnp.where(allowed[None], scores, masked)
        row_max = jnp.max(scores, -1, keepdims=True)
        lifted = jnp.exp(scores - row_max)
        probabilities = (lifted / jnp.sum(lifted, -1, keepdims=True)).astype(jnp.bfloat16)
        return jnp.einsum(
            "hqk,khd->qhd", probabilities, value_rows, preferred_element_type=jnp.float32
        ).astype(jnp.bfloat16)

    heads_out = lax.map(attend, lax.iota(jnp.int32, block_count)).reshape(
        side, col_count, inner_here
    )
    heads_out = jnp.roll(heads_out, lat_offset, axis=0)
    spread = lax.all_to_all(heads_out, "seq", split_axis=0, concat_axis=2, tiled=True)
    grouped = spread.reshape(row_count * col_count, seq_count, inner_here)
    full_out = out_weight[0].reshape(seq_count, inner_here, model_width)
    partial_value = jnp.einsum(
        "tgk,gke->tge", grouped, full_out, preferred_element_type=jnp.float32
    ).astype(jnp.bfloat16)
    branch = jnp.sum(partial_value.astype(jnp.float32), 1).reshape(
        row_count, col_count, model_width
    )
    attention = branch.astype(jnp.bfloat16)
    result = (residual + gate_row * attention.astype(jnp.float32)).astype(jnp.bfloat16)
    carried = passed_along(result, "win", 1)
    joined_back = jnp.concatenate([carried, result], axis=1)
    restored = lax.dynamic_slice_in_dim(joined_back, col_count - lon_offset, col_count, 1)
    handed = passed_along(restored, "segment", 1)
    return handed[None]


def solution(mesh):
    in_specs = (
        P("segment", "seq", "win", None),
        P("segment"),
        P("segment", None),
        P("segment", None, "seq", None),
        P("segment", "seq"),
        P("segment", None, None),
        P("segment", None, None),
        P("segment", None, None),
        P("segment", None, None),
    )
    out_specs = P("segment", "seq", "win", None)
    return jax.shard_map(shards, mesh=mesh, in_specs=in_specs, out_specs=out_specs, check_vma=False)
```

profile of v0, /device:TPU:1, one launch (start us, length us, event | category | flops | bytes accessed | tf_op | source)
XLA Modules:
  0.0 138.1 jit_solution(6706174537842691338)
XLA Ops:
  6.5 19.3 %collective-permute-start = (bf16[2,32,1536]{2,1,0:T(8,128)(2,1)}, bf16[2,32,1536]{2,1,0:T(8,128)(2,1)S(1)}, u32[]{:S(2)}, u32[]{:S(2)}) collective-permute-start(bf16[2,32,1536]{2,1,0:T(8,128)(2,1)} %bitcast.89), channel_id=1, source_target_pairs={{16,0},{32,16},{48,32},{64,48},{80,64},{96,80},{112,96},{128,112},... | collective-permute-start | bytes 589832 | tf_op jit(solution)/shard_map/ppermute | solution.py:13
  25.9 1.3 fusion.41
  29.5 1.1 convolution_reduce_fusion
  30.6 1.1 convolution_reduce_fusion.1
  31.8 1.0 convert_reduce_fusion
  33.0 0.8 fusion.20
  37.4 42.4 %all-gather.2.cloned.1.call-done = bf16[32,32,1536]{2,1,0:T(8,128)(2,1)} async-done(((bf16[2,32,1536]{2,1,0:T(8,128)(2,1)}), bf16[32,32,1536]{2,1,0:T(8,128)(2,1)}) %all-gather.2.cloned.1.call-update) | async-done | bytes 3145744 | tf_op jit(solution)/shard_map/all_gather | solution.py:56
  79.8 3.7 %convolution_bitcast_fusion = f32[32,32,1,288]{3,1,0,2:T(8,128)S(1)} fusion(bf16[32,32,1536]{2,1,0:T(8,128)(2,1)} %all-gather.2.cloned.1.call-done, bf16[1,1536,1,288]{1,3,2,0:T(8,128)(2,1)S(1)} %copy-done), kind=kOutput, calls=%fused_computation.20 | convolution fusion | flops 905969664 | bytes 5210112 | tf_op jit(solution)/shard_map/dot_general | solution.py:57
  84.6 1.7 %fusion.12 = bf16[32,32,1,288]{3,1,0,2:T(8,128)(2,1)S(1)} fusion(s32[]{:T(128)S(6)} %select_n.46, bf16[32,32,1,96]{3,1,0,2:T(8,128)(2,1)S(1)} %get-tuple-element.87, bf16[32,32,1,96]{3,1,0,2:T(8,128)(2,1)S(1)} %get-tuple-element.86, bf16[32,32,1,96]{3,1,0,2:T(8,128)(2,1)S(1)} %slice.44), kind=kLoop, calls=%fused_computation.27 | loop fusion | flops 3538944 | bytes 1179652 | tf_op jit(solution)/shard_map/jit(_roll_dynamic)/concatenate | solution.py:62
  87.1 7.4 %while.10 = (s32[]{:T(128)}, bf16[2,512,1,96]{1,3,2,0:T(8,128)(2,1)S(1)}, s32[2]{0:T(128)S(1)}, pred[1024]{0:T(1024)(128)(4,1)S(1)}, bf16[1024,1,96]{0,2,1:T(8,1...) while((s32[]{:T(128)}, ...), condition=%wide.region_7.8_spmd, body=%wide.region_4.7_spmd.sunk | while | flops 206093312 | bytes 6894271 | solution.py:91
  87.1 0.6 dynamic_slice.96
  88.4 1.2 fusion.50
  90.1 0.6 fusion.52
  92.1 1.2 fusion.50
  93.9 0.6 fusion.52
  94.7 0.9 fusion.22
  95.6 4.8 %all-to-all-start = ((bf16[32,32,96]{2,1,0:T(8,128)(2,1)}), bf16[32,32,96]{2,1,0:T(8,128)(2,1)S(1)}, u32[]{:S(2)}, u32[]{:S(2)}) async-start(bf16[32,32,96]{2,1,0:T(8,128)(2,1)} %fusion.22), calls=%async_computation | async-start | bytes 524288 | tf_op jit(solution)/shard_map/all_to_all | solution.py:95
  100.6 7.0 %all-to-all-done = bf16[32,32,96]{2,1,0:T(8,128)(2,1)S(1)} async-done(((bf16[32,32,96]{2,1,0:T(8,128)(2,1)}), bf16[32,32,96]{2,1,0:T(8,128)(2,1)S(1)}, u32[]{:S(2)}, u32[]{:S(2)}) %all-to-all-start) | async-done | bytes 196640 | tf_op jit(solution)/shard_map/all_to_all | solution.py:95
  107.6 3.3 %fusion.8 = bf16[64,1536]{1,0:T(8,128)(2,1)S(1)} fusion(bf16[64,16,96]{2,0,1:T(8,128)(2,1)S(1)} %bitcast.85, bf16[16,96,1536]{2,1,0:T(8,128)(2,1)} %bitcast.83), kind=kOutput, calls=%fused_computation.19 | convolution fusion | flops 305037312 | bytes 5111808 | tf_op jit(solution)/shard_map/tgk,gke->tge/dot_general | solution.py:98
  111.0 2.4 %collective-permute-start.1 = (bf16[2,32,1536]{2,1,0:T(8,128)(2,1)S(1)}, bf16[2,32,1536]{2,1,0:T(8,128)(2,1)S(1)}, u32[]{:S(2)}, u32[]{:S(2)}) collective-permute-start(bf16[2,32,1536]{2,1,0:T(8,128)(2,1)S(1)} %fusion.21), channel_id=1, source_target_pairs={{496,0},{0,16},{16,32},{32,48},{48,64},{64,80},{80,96},{96,112},{1... | collective-permute-start | bytes 589832 | tf_op jit(solution)/shard_map/ppermute | solution.py:13
  114.5 7.4 %collective-permute-done.1 = bf16[2,32,1536]{2,1,0:T(8,128)(2,1)S(1)} collective-permute-done((bf16[2,32,1536]{2,1,0:T(8,128)(2,1)S(1)}, bf16[2,32,1536]{2,1,0:T(8,128)(2,1)S(1)}, u32[]{:S(2)}, u32[]{:S(2)}) %collective-permute-start.1) | collective-permute-done | bytes 196640 | tf_op jit(solution)/shard_map/ppermute | solution.py:13
  122.0 4.5 %collective-permute-start.2 = (bf16[2,32,1536]{2,1,0:T(8,128)(2,1)S(1)}, bf16[2,32,1536]{2,1,0:T(8,128)(2,1)S(1)}, u32[]{:S(2)}, u32[]{:S(2)}) collective-permute-start(bf16[2,32,1536]{2,1,0:T(8,128)(2,1)S(1)} %fusion.23), channel_id=1, source_target_pairs={{512,0},{0,512},{513,1},{1,513},{514,2},{2,514},{515,3},{3,515},{5... | collective-permute-start | bytes 589832 | tf_op jit(solution)/shard_map/ppermute | solution.py:13
  126.5 4.0 %collective-permute-done.2 = bf16[2,32,1536]{2,1,0:T(8,128)(2,1)S(1)} collective-permute-done((bf16[2,32,1536]{2,1,0:T(8,128)(2,1)S(1)}, bf16[2,32,1536]{2,1,0:T(8,128)(2,1)S(1)}, u32[]{:S(2)}, u32[]{:S(2)}) %collective-permute-start.2) | collective-permute-done | bytes 196640 | tf_op jit(solution)/shard_map/ppermute | solution.py:13
  130.6 0.7 copy.27
  (30 shorter events, 4.4 us)
Async XLA Ops:
  6.5 73.3 %copy-start = (bf16[1,1536,1,288]{1,3,2,0:T(8,128)(2,1)S(1)}, bf16[1,1536,1,288]{1,3,2,0:T(8,128)(2,1)}, u32[]{:S(2)}) copy-start(bf16[1,1536,1,288]{1,3,2,0:T(8,128)(2,1)} %param.14) | copy-start | bytes 2654212
  6.5 73.2 %all-gather.2.cloned.1.call-start = ((), (), s32[]{:S(2)}) async-start(), calls=%async_computation.1 | async-start | bytes 3342336 | tf_op jit(solution)/shard_map/all_gather | solution.py:56
  6.5 25.2 %collective-permute-start = (bf16[2,32,1536]{2,1,0:T(8,128)(2,1)}, bf16[2,32,1536]{2,1,0:T(8,128)(2,1)S(1)}, u32[]{:S(2)}, u32[]{:S(2)}) collective-permute-start(bf16[2,32,1536]{2,1,0:T(8,128)(2,1)} %bitcast.89), channel_id=1, source_target_pairs={{16,0},{32,16},{48,32},{64,48},{80,64},{96,80},{112,96},{128,112},... | collective-permute-start | bytes 589832 | tf_op jit(solution)/shard_map/ppermute | solution.py:13
  87.0 13.4 %copy-start.1 = (f32[1,32,1536]{2,1,0:T(8,128)S(1)}, f32[1,32,1536]{2,1,0:T(8,128)}, u32[]{:S(2)}) copy-start(f32[1,32,1536]{2,1,0:T(8,128)} %param.19) | copy-start | bytes 589828
  95.6 12.0 %all-to-all-start = ((bf16[32,32,96]{2,1,0:T(8,128)(2,1)}), bf16[32,32,96]{2,1,0:T(8,128)(2,1)S(1)}, u32[]{:S(2)}, u32[]{:S(2)}) async-start(bf16[32,32,96]{2,1,0:T(8,128)(2,1)} %fusion.22), calls=%async_computation | async-start | bytes 524288 | tf_op jit(solution)/shard_map/all_to_all | solution.py:95
  111.0 10.9 %collective-permute-start.1 = (bf16[2,32,1536]{2,1,0:T(8,128)(2,1)S(1)}, bf16[2,32,1536]{2,1,0:T(8,128)(2,1)S(1)}, u32[]{:S(2)}, u32[]{:S(2)}) collective-permute-start(bf16[2,32,1536]{2,1,0:T(8,128)(2,1)S(1)} %fusion.21), channel_id=1, source_target_pairs={{496,0},{0,16},{16,32},{32,48},{48,64},{64,80},{80,96},{96,112},{1... | collective-permute-start | bytes 589832 | tf_op jit(solution)/shard_map/ppermute | solution.py:13
  122.0 8.5 %collective-permute-start.2 = (bf16[2,32,1536]{2,1,0:T(8,128)(2,1)S(1)}, bf16[2,32,1536]{2,1,0:T(8,128)(2,1)S(1)}, u32[]{:S(2)}, u32[]{:S(2)}) collective-permute-start(bf16[2,32,1536]{2,1,0:T(8,128)(2,1)S(1)} %fusion.23), channel_id=1, source_target_pairs={{512,0},{0,512},{513,1},{1,513},{514,2},{2,514},{515,3},{3,515},{5... | collective-permute-start | bytes 589832 | tf_op jit(solution)/shard_map/ppermute | solution.py:13
Sparse Core Ops, SparseCore 0:
  34.0 45.7 all-gather.1
where the time goes:
time: 139 us; the launch traced here: 138 us
  waiting for transfers between devices  60.8 us (44%)
  starting transfers between devices  31 us (22%)
  between operations  20.4 us (15%)
  matrix products  13.2 us (9%)
  other arithmetic  7.01 us (5%)
  local copies, waits for them, and re-layouts  4.28 us (3%)
    all_gather x1, waiting for transfers between devices, shards(): shard_rows = lax.all_gather(normed, 'seq', axis=0, tiled=True)  42.4 us
    ppermute x3, starting transfers between devices, passed_along(): return lax.ppermute(block, axis, route)  26.2 us
    ppermute x3, waiting for transfers between devices, passed_along(): return lax.ppermute(block, axis, route)  11.4 us
    all_to_all x1, waiting for transfers between devices, shards(): lax.all_to_all(heads_out, 'seq', split_axis=0, concat_axis=2, tiled=True)  6.99 us
    all_to_all x1, starting transfers between devices, shards(): lax.all_to_all(heads_out, 'seq', split_axis=0, concat_axis=2, tiled=True)  4.78 us
    dot_general x1, matrix products, shards(): jnp.dot(shard_rows.reshape(-1, model_width), weights, preferred_element_t...  3.69 us
    dot_general x1, matrix products, shards(): jnp.einsum('tgk,gke->tge', grouped, full_out, preferred_element_type=jnp....  3.3 us
  transfers between devices with their start and end apart: 5, of which 4 were waited for; matrix products, arithmetic and copies ran while one was open for 3% of the time, Pallas kernels for 0%

commit v1 on v0

v1 whole, which is shorter than its diff:
```python
import functools
import math

import jax
import jax.numpy as jnp
from jax import lax
from jax.experimental import pallas as pl
from jax.experimental.pallas import tpu as pltpu
from jax.sharding import PartitionSpec as P

eps_norm = 1e-06
far_apart = 32768.0
LANES = 128
X_CHIPS = 4
Y_CHIPS = 2
MESH = pl.DeviceIdType.MESH

GROUPS = ((0, 0), (3, 0), (1, 0), (0, 1), (2, 0), (3, 1), (1, 1), (2, 1))


def slot_of(dx, dy, dc):
    return 2 * GROUPS.index((dx % X_CHIPS, dy % Y_CHIPS)) + dc % 2


def back_slot(slot):
    dx, dy = GROUPS[slot // 2]
    return slot_of(-dx, -dy, slot % 2)


def fused(
    wins, chunks,
    tile_ref, level_ref, offset_ref, qkv_ref, scale_ref, out_w_ref, shift_tab, scale_tab, gate_tab,
    out_ref,
    own, beside, tabs, wqkv, wout, tokens, query, key, value, heads, spread, zsend, zrecv, ysend,
    local_sem, in_sem, in_recv, send_sem, recv_sem, head_sem, head_recv, z_sem, z_recv, y_sem, y_recv,
):
    me = lax.axis_index("seq")
    win = lax.axis_index("win")
    segment = lax.axis_index("segment")
    core = lax.rem(me, 2)
    x = lax.rem(me // 2, X_CHIPS)
    y = me // (2 * X_CHIPS)

    def seq_of(slot):
        dx, dy = GROUPS[slot // 2]
        chip = lax.rem(y + dy, Y_CHIPS) * X_CHIPS + lax.rem(x + dx, X_CHIPS)
        return 2 * chip + lax.rem(core + slot % 2, 2)

    def on_seq(slot):
        return {"seq": seq_of(slot)}

    after = {"win": lax.rem(win + 1, wins)}
    before = {"win": lax.rem(win + wins - 1, wins)}
    other = {"segment": 1 - segment}
    right, left, partner, mate = slot_of(1, 0, 0), slot_of(3, 0, 0), slot_of(0, 1, 0), slot_of(0, 0, 1)

    width = own.shape[1]
    half = own.shape[0] // 2
    per_head = wout.shape[1] * 3 // 4
    count = tokens.shape[0]
    rows_in = tokens.shape[1]

    copies = [pltpu.make_async_copy(tile_ref, own, local_sem.at[0])]
    for i, tab in enumerate((shift_tab, scale_tab, gate_tab)):
        copies.append(pltpu.make_async_copy(tab, tabs.at[i], local_sem.at[1 + i]))
    for i in range(3):
        copies.append(
            pltpu.make_async_copy(
                qkv_ref.at[pl.ds(i * per_head, per_head)],
                wqkv.at[pl.ds(i * LANES, per_head)],
                local_sem.at[4 + i],
            )
        )
    for copy in copies:
        copy.start()
    out_copies = []
    for slot in range(count):
        first = pl.multiple_of(seq_of(slot) * per_head, per_head)
        copy = pltpu.make_async_copy(
            out_w_ref.at[pl.ds(first, per_head)],
            wout.at[slot, pl.ds(0, per_head)],
            local_sem.at[7 + slot],
        )
        copy.start()
        out_copies.append(copy)

    barrier = pltpu.get_barrier_semaphore()
    greeted = [after, before, other] + [on_seq(s) for s in (right, left, partner, mate)]
    for device in greeted:
        pl.semaphore_signal(barrier, inc=1, device_id=device, device_id_type=MESH)
    pl.semaphore_wait(barrier, len(greeted))

    sent = []

    def push(src, dst, send, recv, device):
        copy = pltpu.make_async_remote_copy(
            src_ref=src, dst_ref=dst, send_sem=send, recv_sem=recv, device_id=device, device_id_type=MESH
        )
        copy.start()
        sent.append(copy)

    def arrived(ref, sem):
        pltpu.make_async_remote_copy(
            src_ref=ref, dst_ref=ref, send_sem=send_sem.at[0], recv_sem=sem, device_id=after, device_id_type=MESH
        ).wait_recv()

    copies[0].wait()
    for h in range(2):
        part = pl.ds(h * half, half)
        push(own.at[part], beside.at[part], in_sem.at[h], in_recv.at[h], before)

    for i in range(3):
        wqkv[pl.ds(i * LANES + per_head, LANES - per_head), :] = jnp.zeros((LANES - per_head, width), wqkv.dtype)
    for slot in range(count):
        wout[slot, pl.ds(per_head, LANES - per_head), :] = jnp.zeros((LANES - per_head, width), wout.dtype)
    level = level_ref[0]
    lat_offset = offset_ref[0, 0]
    lon_offset = offset_ref[0, 1]
    for i in range(3):
        copies[1 + i].wait()
    shift_row = tabs[0, pl.ds(level, 1), :]
    scale_row = tabs[1, pl.ds(level, 1), :]
    gate_row = tabs[2, pl.ds(level, 1), :]
    kept = lax.broadcasted_iota(jnp.int32, (half, 1), 0) >= lon_offset

    counter = [0]

    def send_block(src_slot, h, device_slot, dst_slot):
        part = pl.ds(h * half, half)
        push(
            tokens.at[src_slot, part], tokens.at[dst_slot, part],
            send_sem.at[counter[0]], recv_sem.at[dst_slot, h], on_seq(device_slot),
        )
        counter[0] += 1

    for h in range(2):
        part = pl.ds(h * half, half)
        arrived(beside.at[part], in_recv.at[h])
        rows = jnp.where(kept, own[part, :].astype(jnp.float32), beside[part, :].astype(jnp.float32))
        centred = rows - jnp.mean(rows, -1, keepdims=True)
        variance = jnp.mean(centred * centred, -1, keepdims=True)
        normed = centred * lax.rsqrt(variance + eps_norm) * scale_row + shift_row
        tokens[0, part, :] = normed.astype(tokens.dtype)
        send_block(0, h, right, left)
        send_block(0, h, left, right)
        send_block(0, h, partner, partner)
        send_block(0, h, mate, mate)

    def take(slot, h):
        arrived(tokens.at[slot, pl.ds(h * half, half)], recv_sem.at[slot, h])

    def take_and_share(slot, h):
        take(slot, h)
        send_block(slot, h, mate, slot + 1)

    lane = lax.broadcasted_iota(jnp.int32, (2 * rows_in, LANES), 1)
    index = lax.broadcasted_iota(jnp.int32, (2 * rows_in, LANES), 0)
    second = (index // rows_in).astype(jnp.int32)
    parity = lax.rem(index // half, 2)

    def project(g):
        for h in range(2):
            take(2 * g + 1, h)
        block = tokens[pl.ds(2 * g, 2)].reshape(2 * rows_in, width)
        mixed = lax.dot_general(
            block, wqkv[...], (((1,), (1,)), ((), ())), preferred_element_type=jnp.float32
        )
        q = mixed[:, :LANES]
        k = mixed[:, LANES : 2 * LANES]
        v = mixed[:, 2 * LANES :]
        q = q * lax.rsqrt(jnp.sum(q * q, -1, keepdims=True) + eps_norm)
        k = k * lax.rsqrt(jnp.sum(k * k, -1, keepdims=True) + eps_norm)
        owner = jnp.where(second == 0, seq_of(2 * g), seq_of(2 * g + 1))
        late = 2 * owner + parity >= lat_offset
        q = jnp.where(lane == per_head, jnp.where(late, 1.0, 0.0), q)
        q = jnp.where(lane == per_head + 1, jnp.where(late, 0.0, 1.0), q)
        k = jnp.where(lane == per_head, jnp.where(late, 0.0, -far_apart), k)
        k = jnp.where(lane == per_head + 1, jnp.where(late, -far_apart, 0.0), k)
        v = jnp.where(lane == per_head, 1.0, v)
        at = pl.ds(g * 2 * rows_in, 2 * rows_in)
        query[at, :] = q.astype(query.dtype)
        key[at, :] = k.astype(key.dtype)
        value[at, :] = v.astype(value.dtype)

    far, partner_left, partner_right, partner_far = slot_of(2, 0, 0), slot_of(3, 1, 0), slot_of(1, 1, 0), slot_of(2, 1, 0)

    for i in range(3):
        copies[4 + i].wait()
    project(0)
    take_and_share(left, 0)
    send_block(left, 0, right, far)
    take_and_share(partner, 0)
    send_block(partner, 0, right, partner_left)
    send_block(partner, 0, left, partner_right)
    take_and_share(right, 0)
    take_and_share(right, 1)
    send_block(right, 1, left, far)
    take_and_share(partner, 1)
    send_block(partner, 1, right, partner_left)
    send_block(partner, 1, left, partner_right)
    take_and_share(left, 1)
    project(1)
    take_and_share(far, 0)
    send_block(far, 0, partner, partner_far)
    project(2)
    take_and_share(far, 1)
    send_block(far, 1, partner, partner_far)
    take_and_share(partner_right, 0)
    project(3)
    take_and_share(partner_left, 0)
    project(4)
    take_and_share(partner_far, 0)
    take_and_share(partner_left, 1)
    take_and_share(partner_right, 1)
    take_and_share(partner_far, 1)
    project(5)
    project(6)
    project(7)

    factor = scale_ref[0, 0] * math.log2(math.e)
    for g in reversed(range(len(GROUPS))):
        scores = lax.dot_general(
            query[pl.ds(g * 2 * rows_in, 2 * rows_in), :], key[...], (((1,), (1,)), ((), ())),
            preferred_element_type=jnp.float32,
        )
        lifted = jnp.exp2((scores - jnp.max(scores, -1, keepdims=True)) * factor)
        mixed = jnp.dot(lifted.astype(jnp.bfloat16), value[...], preferred_element_type=jnp.float32)
        mixed = mixed / mixed[:, per_head : per_head + 1]
        heads[pl.ds(2 * g, 2)] = mixed.astype(heads.dtype).reshape(2, rows_in, LANES)
        for slot in (2 * g, 2 * g + 1):
            if slot:
                to = back_slot(slot)
                push(heads.at[slot], spread.at[to], head_sem.at[slot], head_recv.at[to], on_seq(slot))
    spread[0] = heads[0]

    for copy in out_copies:
        copy.wait()
    for slot in range(1, count):
        arrived(spread.at[slot], head_recv.at[slot])
    gathered = jnp.concatenate([spread[slot] for slot in range(count)], axis=-1)
    piece = width // chunks
    for n in range(chunks):
        columns = pl.ds(n * piece, piece)
        attention = jnp.dot(
            gathered, wout[:, :, columns].reshape(count * LANES, piece), preferred_element_type=jnp.float32
        )
        zsend[n] = attention.astype(zsend.dtype)
        push(zsend.at[n], zrecv.at[n], z_sem.at[n], z_recv.at[n], after)
    column = lax.broadcasted_iota(jnp.int32, (2 * half, 1), 0)
    kept = jnp.where(column >= half, column - half, column) >= lon_offset
    for n in range(chunks):
        columns = pl.ds(n * piece, piece)
        arrived(zrecv.at[n], z_recv.at[n])
        attention = jnp.where(kept, zsend[n].astype(jnp.float32), zrecv[n].astype(jnp.float32))
        finished = own[:, columns].astype(jnp.float32) + gate_row[:, n * piece : (n + 1) * piece] * attention
        ysend[n] = finished.astype(ysend.dtype)
        push(ysend.at[n], out_ref.at[:, columns], y_sem.at[n], y_recv.at[n], other)
    for n in range(chunks):
        arrived(out_ref.at[:, pl.ds(n * piece, piece)], y_recv.at[n])
    for copy in sent:
        copy.wait_send()


def shards(
    latents, timesteps, offsets, qkv_weight, logit_scale, out_weight, mod_shift, mod_scale, mod_gate
):
    _, row_count, col_count, width = latents.shape
    head_size = qkv_weight.shape[3] // 3
    wins, seq = lax.axis_size("win"), lax.axis_size("seq")
    here = row_count * col_count
    steps = mod_shift.shape[1]
    chunks = 4 if width % 512 == 0 else 2
    piece = width // chunks
    bf16 = jnp.bfloat16
    any_space = pl.BlockSpec(memory_space=pl.ANY)
    scalars = pl.BlockSpec(memory_space=pltpu.SMEM)
    dma = pltpu.SemaphoreType.DMA
    result = pl.pallas_call(
        functools.partial(fused, wins, chunks),
        out_shape=jax.ShapeDtypeStruct((here, width), bf16),
        in_specs=[any_space, scalars, scalars, any_space, scalars] + [any_space] * 4,
        out_specs=any_space,
        scratch_shapes=[
            pltpu.VMEM((here, width), bf16),
            pltpu.VMEM((here, width), bf16),
            pltpu.VMEM((3, steps, width), jnp.float32),
            pltpu.VMEM((3 * LANES, width), bf16),
            pltpu.VMEM((seq, LANES, width), bf16),
            pltpu.VMEM((seq, here, width), bf16),
            pltpu.VMEM((seq * here, LANES), bf16),
            pltpu.VMEM((seq * here, LANES), bf16),
            pltpu.VMEM((seq * here, LANES), bf16),
            pltpu.VMEM((seq, here, LANES), bf16),
            pltpu.VMEM((seq, here, LANES), bf16),
            pltpu.VMEM((chunks, here, piece), bf16),
            pltpu.VMEM((chunks, here, piece), bf16),
            pltpu.VMEM((chunks, here, piece), bf16),
            dma((7 + seq,)),
            dma((2,)),
            dma((2,)),
            dma((32,)),
            dma((seq, 2)),
            dma((seq,)),
            dma((seq,)),
            dma((chunks,)),
            dma((chunks,)),
            dma((chunks,)),
            dma((chunks,)),
        ],
        compiler_params=pltpu.CompilerParams(
            collective_id=0, has_side_effects=True, vmem_limit_bytes=60 * 1024 * 1024
        ),
    )(
        latents.reshape(here, width),
        timesteps,
        offsets,
        qkv_weight[0, :, 0, :].T,
        logit_scale,
        out_weight[0],
        mod_shift[0],
        mod_scale[0],
        mod_gate[0],
    )
    return result.reshape(1, row_count, col_count, width)


def solution(mesh):
    in_specs = (
        P("segment", "seq", "win", None),
        P("segment"),
        P("segment", None),
        P("segment", None, "seq", None),
        P("segment", "seq"),
        P("segment", None, None),
        P("segment", None, None),
        P("segment", None, None),
        P("segment", None, None),
    )
    out_specs = P("segment", "seq", "win", None)
    return jax.shard_map(shards, mesh=mesh, in_specs=in_specs, out_specs=out_specs, check_vma=False)
```

time: 139 us -> 64.8 us (0.47)
  Pallas kernels: 0 us -> 61.7 us
  waiting for transfers between devices: 60.8 us -> 0 us
  starting transfers between devices: 31 us -> 0 us
  between operations: 20.4 us -> 1.3 us
  matrix products: 13.2 us -> 0 us
  other arithmetic: 7.01 us -> 0 us
  local copies, waits for them, and re-layouts: 4.28 us -> 1.62 us
    pallas_call x0 -> x1, Pallas kernels: none -> 61.7 us  [shards(): pl.pallas_call(functools.partial(fused, wins, chunks), out_shape=jax.Shap...]
    all_gather x1 -> x0, waiting for transfers between devices: 42.4 us -> none  [shards(): shard_rows = lax.all_gather(normed, 'seq', axis=0, tiled=True)]
    ppermute x3 -> x0, starting transfers between devices: 26.2 us -> none  [passed_along(): return lax.ppermute(block, axis, route)]
    dot_general x9 -> x0, matrix products: 13.2 us -> none  [the longest x1 3.69 us: shards(): jnp.dot(shard_rows.reshape(-1, model_width), weights, preferred_element_t...]
    ppermute x3 -> x0, waiting for transfers between devices: 11.4 us -> none  [passed_along(): return lax.ppermute(block, axis, route)]
    all_to_all x1 -> x0, waiting for transfers between devices: 6.99 us -> none  [shards(): lax.all_to_all(heads_out, 'seq', split_axis=0, concat_axis=2, tiled=True)]
    all_to_all x1 -> x0, starting transfers between devices: 4.78 us -> none  [shards(): lax.all_to_all(heads_out, 'seq', split_axis=0, concat_axis=2, tiled=True)]
    concatenate x3 -> x0, other arithmetic: 2.81 us -> none  [the longest x1 1.74 us: shards(): window = jnp.roll(gathered, -lat_offset, axis=0)]
  transfers between devices with their start and end apart: 5 -> 0, of which waited for: 4 -> 0; matrix products, arithmetic and copies ran while one was open for 3% -> 0% of each run, Pallas kernels for 0% -> 0%
where the time goes in v1:
time: 64.8 us; the launch traced here: 64.6 us
  Pallas kernels  61.7 us (95%)
  local copies, waits for them, and re-layouts  1.62 us (2%)
  between operations  1.3 us (2%)
    pallas_call x1, Pallas kernels, shards(): pl.pallas_call(functools.partial(fused, wins, chunks), out_shape=jax.Shap...  61.7 us
    unnamed x1, local copies, waits for them, and re-layouts  1.62 us

profile of v1, /device:TPU:1, one launch (start us, length us, event | category | flops | bytes accessed | tf_op | source)
XLA Modules:
  0.0 64.6 jit_solution(6520415209874252680)
XLA Ops:
  1.3 61.7 %shard_map.91 = bf16[64,1536]{1,0:T(8,128)(2,1)} custom-call(bf16[64,1536]{1,0:T(8,128)(2,1)} %bitcast.12, s32[1]{0:T(128)S(6)} %copy.11.level_ref, s32[1,2]{1,0:T(1,128)} %offset_ref.1, bf16[288,1536]{1,0:T(8,128)(2,1)} %bitcast.10, f32[1,1]{1,0:T(1,128)S(6)} %copy.12.scale_ref, bf16[1536,1536]{1,0:T(8,128)(2,1)} %bitcast.9, f32[32,1536]{1,0:T(8,128)} %bitcast.13, ...), custom_call_target="tpu_custom_call" | custom-call | tf_op jit(solution)/shard_map/pallas_call | solution.py:278
  63.0 1.6 %copy.13 = bf16[1,2,32,1536]{3,2,1,0:T(8,128)(2,1)} copy(bf16[1,2,32,1536]{3,2,1,0:T(8,128)(2,1)} %bitcast.11) | data formatting | bytes 393216

commit v2 on v1

v2 whole, which is shorter than its diff:
```python
import functools
import math

import jax
import jax.numpy as jnp
from jax import lax
from jax.experimental import pallas as pl
from jax.experimental.pallas import tpu as pltpu
from jax.sharding import PartitionSpec as P

eps_norm = 1e-06
far_apart = 32768.0
LANES = 128
X_CHIPS = 4
Y_CHIPS = 2
PIECES = 4
EARLY = 10
MESH = pl.DeviceIdType.MESH

GROUPS = ((0, 0), (3, 0), (1, 0), (0, 1), (2, 0), (3, 1), (1, 1), (2, 1))


def slot_of(dx, dy, dc):
    return 2 * GROUPS.index((dx % X_CHIPS, dy % Y_CHIPS)) + dc % 2


def back_slot(slot):
    dx, dy = GROUPS[slot // 2]
    return slot_of(-dx, -dy, slot % 2)


def fused(
    wins, chunks,
    tile_ref, level_hbm, offset_hbm, qkv_ref, scale_hbm, out_w_ref, shift_tab, scale_tab, gate_tab,
    out_ref,
    level_ref, offset_ref, scale_ref,
    own, beside, tabs, wqkv, wmix, wout, tokens, late_tokens, query, key, value, heads, spread, mine, zsend, zrecv, ysend,
    local_sem, in_sem, in_recv, send_sem, recv_sem, head_sem, head_recv, z_sem, z_recv, y_sem, y_recv,
):
    me = lax.axis_index("seq")
    win = lax.axis_index("win")
    segment = lax.axis_index("segment")
    core = lax.rem(me, 2)
    x = lax.rem(me // 2, X_CHIPS)
    y = me // (2 * X_CHIPS)

    def seq_of(slot):
        dx, dy = GROUPS[slot // 2]
        chip = lax.rem(y + dy, Y_CHIPS) * X_CHIPS + lax.rem(x + dx, X_CHIPS)
        return 2 * chip + lax.rem(core + slot % 2, 2)

    def on_seq(slot):
        return {"seq": seq_of(slot)}

    right, left, partner, mate = slot_of(1, 0, 0), slot_of(3, 0, 0), slot_of(0, 1, 0), slot_of(0, 0, 1)
    far, partner_left, partner_right, partner_far = slot_of(2, 0, 0), slot_of(3, 1, 0), slot_of(1, 1, 0), slot_of(2, 1, 0)
    after = {"win": lax.rem(win + 1, wins)}
    before = {"win": lax.rem(win + wins - 1, wins)}
    other = {"segment": 1 - segment}
    across = {"segment": 1 - segment, "seq": seq_of(partner)}

    width = own.shape[1]
    here = own.shape[0]
    half = here // 2
    low = half // 2
    unit = here // PIECES
    per_head = LANES * 3 // 4
    count = spread.shape[0]

    copies = [pltpu.make_async_copy(tile_ref, own, local_sem.at[0])]
    for i, tab in enumerate((shift_tab, scale_tab, gate_tab)):
        copies.append(pltpu.make_async_copy(tab, tabs.at[i], local_sem.at[1 + i]))
    for i in range(3):
        copies.append(
            pltpu.make_async_copy(
                qkv_ref.at[pl.ds(i * per_head, per_head)],
                wqkv.at[pl.ds(i * LANES, per_head)],
                local_sem.at[4 + i],
            )
        )
    copies.append(pltpu.make_async_copy(level_hbm, level_ref, local_sem.at[7]))
    copies.append(pltpu.make_async_copy(offset_hbm, offset_ref, local_sem.at[8]))
    copies.append(pltpu.make_async_copy(scale_hbm, scale_ref, local_sem.at[9]))
    for copy in copies:
        copy.start()

    barrier = pltpu.get_barrier_semaphore()
    greeted = [after, before, across] + [on_seq(s) for s in (right, left, partner, mate)]
    for device in greeted:
        pl.semaphore_signal(barrier, inc=1, device_id=device, device_id_type=MESH)

    out_copies = []
    for slot in range(count):
        first = pl.multiple_of(seq_of(slot) * per_head, per_head)
        copy = pltpu.make_async_copy(
            out_w_ref.at[pl.ds(first, per_head)],
            wout.at[pl.ds(slot * per_head, per_head)],
            local_sem.at[10 + slot],
        )
        copy.start()
        out_copies.append(copy)
    copies[0].wait()
    pl.semaphore_wait(barrier, len(greeted))

    sent = []

    def push(src, dst, send, recv, device):
        copy = pltpu.make_async_remote_copy(
            src_ref=src, dst_ref=dst, send_sem=send, recv_sem=recv, device_id=device, device_id_type=MESH
        )
        copy.start()
        sent.append(copy)

    def arrived(ref, sem):
        pltpu.make_async_remote_copy(
            src_ref=ref, dst_ref=ref, send_sem=send_sem.at[0], recv_sem=sem, device_id=after, device_id_type=MESH
        ).wait_recv()

    sides = ((0, before), (1, after))
    for h in range(2):
        for s, device in sides:
            part = pl.ds(h * half + s * low, low)
            push(own.at[part], beside.at[part], in_sem.at[h, s], in_recv.at[h, s], device)

    for i in range(3):
        wqkv[pl.ds(i * LANES + per_head, LANES - per_head), :] = jnp.zeros((LANES - per_head, width), wqkv.dtype)
    for i in range(3):
        copies[4 + i].wait()
    wmix[...] = wqkv[...].T
    for copy in copies[7:]:
        copy.wait()
    level = level_ref[0]
    lat_offset = offset_ref[0, 0]
    lon_offset = offset_ref[0, 1]
    for i in range(3):
        copies[1 + i].wait()
    shift_row = tabs[0, pl.ds(level, 1), :]
    scale_row = tabs[1, pl.ds(level, 1), :]
    gate_row = tabs[2, pl.ds(level, 1), :]
    column = lax.broadcasted_iota(jnp.int32, (half, 1), 0)
    low_end = jnp.where(lon_offset <= low, lon_offset, 0)
    high_start = jnp.where(lon_offset <= low, half, lon_offset)

    def taken(column):
        return jnp.logical_or(column < low_end, column >= high_start)

    counter = [0]

    def piece(slot, p):
        if slot < EARLY:
            return tokens.at[slot, pl.ds(p * unit, unit)]
        return late_tokens.at[p, slot - EARLY]

    def send_piece(src_slot, p, device_slot, dst_slot):
        push(
            piece(src_slot, p), piece(dst_slot, p),
            send_sem.at[counter[0]], recv_sem.at[dst_slot, p], on_seq(device_slot),
        )
        counter[0] += 1

    for h in range(2):
        part = pl.ds(h * half, half)
        for s, _ in sides:
            arrived(beside.at[pl.ds(h * half + s * low, low)], in_recv.at[h, s])
        rows = jnp.where(taken(column), beside[part, :].astype(jnp.float32), own[part, :].astype(jnp.float32))
        centred = rows - jnp.mean(rows, -1, keepdims=True)
        variance = jnp.mean(centred * centred, -1, keepdims=True)
        normed = centred * lax.rsqrt(variance + eps_norm) * scale_row + shift_row
        tokens[0, part, :] = normed.astype(tokens.dtype)
        for p in (2 * h, 2 * h + 1):
            send_piece(0, p, partner, partner)
            if p < 3:
                send_piece(0, p, right, left)
            send_piece(0, p, left, right)
        for p in (2 * h, 2 * h + 1):
            send_piece(0, p, mate, mate)

    def take(slot, p):
        arrived(piece(slot, p), recv_sem.at[slot, p])

    def share(slot, p):
        send_piece(slot, p, mate, slot + 1)

    def project(block, owners, parities, start):
        size = block.shape[0]
        each = size // len(owners)
        mixed = jnp.dot(block, wmix[...], preferred_element_type=jnp.float32)
        q = mixed[:, :LANES]
        k = mixed[:, LANES : 2 * LANES]
        v = mixed[:, 2 * LANES :]
        q = q * lax.rsqrt(jnp.sum(q * q, -1, keepdims=True) + eps_norm)
        k = k * lax.rsqrt(jnp.sum(k * k, -1, keepdims=True) + eps_norm)
        lane = lax.broadcasted_iota(jnp.int32, (size, LANES), 1)
        index = lax.broadcasted_iota(jnp.int32, (size, LANES), 0)
        row = jnp.zeros((size, LANES), jnp.int32)
        for i, (slot, parity) in enumerate(zip(owners, parities)):
            row = jnp.where(index >= i * each, 2 * seq_of(slot) + parity, row)
        late = row >= lat_offset
        q = jnp.where(lane == per_head, jnp.where(late, 1.0, 0.0), q)
        q = jnp.where(lane == per_head + 1, jnp.where(late, 0.0, 1.0), q)
        k = jnp.where(lane == per_head, jnp.where(late, 0.0, -far_apart), k)
        k = jnp.where(lane == per_head + 1, jnp.where(late, -far_apart, 0.0), k)
        v = jnp.where(lane == per_head, 1.0, v)
        at = pl.ds(start, size)
        query[at, :] = q.astype(query.dtype)
        key[at, :] = k.astype(key.dtype)
        value[at, :] = v.astype(value.dtype)

    def project_group(g):
        for p in range(PIECES):
            take(2 * g + 1, p)
        block = tokens[pl.ds(2 * g, 2)].reshape(2 * here, width)
        project(block, (2 * g, 2 * g, 2 * g + 1, 2 * g + 1), (0, 1, 0, 1), g * 2 * here)

    late_slots = tuple(range(EARLY, count))
    late_size = len(late_slots) * unit

    def project_late(p):
        for slot in late_slots[1::2]:
            take(slot, p)
        block = late_tokens[p].reshape(late_size, width)
        project(block, late_slots, (p // 2,) * len(late_slots), EARLY * here + p * late_size)

    take(left, 0)
    send_piece(left, 0, right, far)
    send_piece(0, 3, right, left)
    share(left, 0)
    take(partner, 0)
    share(partner, 0)
    take(right, 0)
    share(right, 0)
    project_group(0)
    take(right, 1)
    send_piece(right, 1, left, far)
    share(right, 1)
    send_piece(partner, 0, left, partner_right)
    take(left, 1)
    share(left, 1)
    take(partner, 1)
    share(partner, 1)
    take(left, 2)
    send_piece(left, 2, right, far)
    share(left, 2)
    send_piece(partner, 0, right, partner_left)
    send_piece(partner, 1, right, partner_left)
    take(right, 2)
    share(right, 2)
    take(partner, 2)
    share(partner, 2)
    take(far, 0)
    send_piece(far, 0, partner, partner_far)
    share(far, 0)
    take(right, 3)
    send_piece(right, 3, left, far)
    share(right, 3)
    send_piece(partner, 1, left, partner_right)
    send_piece(partner, 2, left, partner_right)
    send_piece(partner, 2, right, partner_left)
    take(left, 3)
    share(left, 3)
    take(partner, 3)
    share(partner, 3)
    send_piece(partner, 3, right, partner_left)
    send_piece(partner, 3, left, partner_right)
    take(far, 1)
    send_piece(far, 1, partner, partner_far)
    share(far, 1)
    project_group(1)
    take(far, 2)
    send_piece(far, 2, partner, partner_far)
    share(far, 2)
    project_group(2)
    take(far, 3)
    send_piece(far, 3, partner, partner_far)
    share(far, 3)
    late_firsts = (partner_right, partner_left, partner_far)
    def take_late(p):
        for slot in late_firsts:
            take(slot, p)
            share(slot, p)

    project_group(3)
    take_late(0)
    project_group(4)
    take_late(1)
    project_late(0)
    take_late(2)
    project_late(1)
    take_late(3)
    project_late(2)
    project_late(3)

    factor = scale_ref[0, 0] * math.log2(math.e)

    def attend(start, size):
        scores = lax.dot_general(
            query[pl.ds(start, size), :], key[...], (((1,), (1,)), ((), ())), preferred_element_type=jnp.float32
        )
        lifted = jnp.exp2((scores - jnp.max(scores, -1, keepdims=True)) * factor)
        mixed = jnp.dot(lifted.astype(jnp.bfloat16), value[...], preferred_element_type=jnp.float32)
        return (mixed / mixed[:, per_head : per_head + 1]).astype(heads.dtype)

    def deliver(slot):
        if slot:
            to = back_slot(slot)
            push(heads.at[slot], spread.at[to], head_sem.at[slot], head_recv.at[to], on_seq(slot))

    mixed = attend(EARLY * here, late_size * PIECES)
    for i, slot in enumerate(late_slots):
        for p in range(PIECES):
            first = p * late_size + i * unit
            heads[slot, pl.ds(p * unit, unit), :] = mixed[first : first + unit]
    for slot in reversed(late_slots):
        deliver(slot)
    middle = 4
    for slots in (range(middle, EARLY), range(middle)):
        mixed = attend(slots[0] * here, len(slots) * here)
        heads[pl.ds(slots[0], len(slots))] = mixed.reshape(len(slots), here, LANES)
        for slot in reversed(slots):
            deliver(slot)
    spread[0] = heads[0]

    for copy in out_copies:
        copy.wait()
    for slot in range(1, count):
        arrived(spread.at[slot], head_recv.at[slot])
    gathered = jnp.concatenate([spread[slot][:, :per_head] for slot in range(count)], axis=-1)
    span = width // chunks
    for n in range(chunks):
        columns = pl.ds(n * span, span)
        attention = jnp.dot(
            gathered, wout[:, columns], preferred_element_type=jnp.float32
        ).astype(mine.dtype)
        mine[n] = attention
        for s, device in ((0, after), (1, before)):
            first = s * low
            zsend[n, s] = jnp.concatenate([attention[first : first + low], attention[half + first : half + first + low]])
            push(zsend.at[n, s], zrecv.at[n, s], z_sem.at[n, s], z_recv.at[n, s], device)
    column = lax.broadcasted_iota(jnp.int32, (here, 1), 0)
    given = taken(jnp.where(column >= half, column - half, column))
    for n in range(chunks):
        columns = pl.ds(n * span, span)
        for s, _ in sides:
            arrived(zrecv.at[n, s], z_recv.at[n, s])
        lows, highs = zrecv[n, 0], zrecv[n, 1]
        theirs = jnp.concatenate([lows[:low], highs[:low], lows[low:], highs[low:]])
        attention = jnp.where(given, theirs.astype(jnp.float32), mine[n].astype(jnp.float32))
        finished = own[:, columns].astype(jnp.float32) + gate_row[:, n * span : (n + 1) * span] * attention
        ysend[n] = finished.astype(ysend.dtype)
        push(ysend.at[n], out_ref.at[:, columns], y_sem.at[n], y_recv.at[n], other)
    for n in range(chunks):
        arrived(out_ref.at[:, pl.ds(n * span, span)], y_recv.at[n])
    for copy in sent:
        copy.wait_send()


def shards(
    latents, timesteps, offsets, qkv_weight, logit_scale, out_weight, mod_shift, mod_scale, mod_gate
):
    _, row_count, col_count, width = latents.shape
    wins, seq = lax.axis_size("win"), lax.axis_size("seq")
    here = row_count * col_count
    unit = here // PIECES
    steps = mod_shift.shape[1]
    chunks = 3 if width % 384 == 0 else 2
    span = width // chunks
    bf16 = jnp.bfloat16
    in_hbm = pl.BlockSpec(memory_space=pltpu.HBM)
    dma = pltpu.SemaphoreType.DMA
    result = pl.pallas_call(
        functools.partial(fused, wins, chunks),
        out_shape=pltpu.VMEM((here, width), bf16),
        in_specs=[in_hbm] * 9,
        out_specs=pl.BlockSpec(memory_space=pltpu.VMEM),
        scratch_shapes=[
            pltpu.SMEM((1,), jnp.int32),
            pltpu.SMEM((1, 2), jnp.int32),
            pltpu.SMEM((1, 1), jnp.float32),
            pltpu.VMEM((here, width), bf16),
            pltpu.VMEM((here, width), bf16),
            pltpu.VMEM((3, steps, width), jnp.float32),
            pltpu.VMEM((3 * LANES, width), bf16),
            pltpu.VMEM((width, 3 * LANES), bf16),
            pltpu.VMEM((seq * (LANES * 3 // 4), width), bf16),
            pltpu.VMEM((EARLY, here, width), bf16),
            pltpu.VMEM((PIECES, seq - EARLY, unit, width), bf16),
            pltpu.VMEM((seq * here, LANES), bf16),
            pltpu.VMEM((seq * here, LANES), bf16),
            pltpu.VMEM((seq * here, LANES), bf16),
            pltpu.VMEM((seq, here, LANES), bf16),
            pltpu.VMEM((seq, here, LANES), bf16),
            pltpu.VMEM((chunks, here, span), bf16),
            pltpu.VMEM((chunks, 2, here // 2, span), bf16),
            pltpu.VMEM((chunks, 2, here // 2, span), bf16),
            pltpu.VMEM((chunks, here, span), bf16),
            dma((10 + seq,)),
            dma((2, 2)),
            dma((2, 2)),
            dma((64,)),
            dma((seq, PIECES)),
            dma((seq,)),
            dma((seq,)),
            dma((chunks, 2)),
            dma((chunks, 2)),
            dma((chunks,)),
            dma((chunks,)),
        ],
        compiler_params=pltpu.CompilerParams(
            collective_id=0, has_side_effects=True, vmem_limit_bytes=56 * 1024 * 1024
        ),
    )(
        latents.reshape(here, width),
        timesteps,
        offsets,
        qkv_weight[0, :, 0, :].T,
        logit_scale,
        out_weight[0],
        mod_shift[0],
        mod_scale[0],
        mod_gate[0],
    )
    return result.reshape(1, row_count, col_count, width)


def solution(mesh):
    in_specs = (
        P("segment", "seq", "win", None),
        P("segment"),
        P("segment", None),
        P("segment", None, "seq", None),
        P("segment", "seq"),
        P("segment", None, None),
        P("segment", None, None),
        P("segment", None, None),
        P("segment", None, None),
    )
    out_specs = P("segment", "seq", "win", None)
    return jax.shard_map(shards, mesh=mesh, in_specs=in_specs, out_specs=out_specs, check_vma=False)
```

time: 64.8 us -> 59.4 us (0.917)
  Pallas kernels: 61.7 us -> 57.2 us
  local copies, waits for them, and re-layouts: 1.62 us -> 0.68 us
    pallas_call x1, Pallas kernels: 61.7 us -> 57.2 us  [shards(): pl.pallas_call(functools.partial(fused, wins, chunks), out_shape=pltpu.VM...]
    unnamed x1, local copies, waits for them, and re-layouts: 1.62 us -> 0.68 us
where the time goes in v2:
time: 59.4 us; the launch traced here: 59.2 us
  Pallas kernels  57.2 us (96%)
  between operations  1.3 us (2%)
  local copies, waits for them, and re-layouts  0.68 us (1%)
    pallas_call x1, Pallas kernels, shards(): pl.pallas_call(functools.partial(fused, wins, chunks), out_shape=pltpu.VM...  57.2 us

profile of v2, /device:TPU:1, one launch (start us, length us, event | category | flops | bytes accessed | tf_op | source)
XLA Modules:
  0.0 59.2 jit_solution(9465682217627424889)
XLA Ops:
  1.3 57.2 %shard_map.91 = bf16[64,1536]{1,0:T(8,128)(2,1)S(1)} custom-call(bf16[64,1536]{1,0:T(8,128)(2,1)} %bitcast.12, s32[1]{0:T(128)S(6)} %copy.12.level_hbm, s32[1,2]{1,0:T(1,128)} %offset_hbm.1, bf16[288,1536]{1,0:T(8,128)(2,1)} %bitcast.11, f32[1,1]{1,0:T(1,128)S(6)} %copy.13.scale_hbm, bf16[1536,1536]{1,0:T(8,128)(2,1)} %bitcast.10, f32[32,1536]{1,0:T(8,128)} %bitcast.13, ...), custom_call_target="tpu_custom_call" | custom-call | tf_op jit(solution)/shard_map/pallas_call | solution.py:370
  58.5 0.7 %copy.11 = bf16[1,2,32,1536]{3,2,1,0:T(8,128)(2,1)} copy(bf16[1,2,32,1536]{3,2,1,0:T(8,128)(2,1)S(1)} %bitcast.9) | data formatting | bytes 393216

commit v3 on v2

v3 whole, which is shorter than its diff:
```python
import functools
import math

import jax
import jax.numpy as jnp
from jax import lax
from jax.experimental import pallas as pl
from jax.experimental.pallas import tpu as pltpu
from jax.sharding import PartitionSpec as P

eps_norm = 1e-06
far_apart = 32768.0
LANES = 128
X_CHIPS = 4
Y_CHIPS = 2
PIECES = 4
EARLY = 10
MESH = pl.DeviceIdType.MESH

GROUPS = ((0, 0), (3, 0), (1, 0), (0, 1), (2, 0), (3, 1), (1, 1), (2, 1))


def slot_of(dx, dy, dc):
    return 2 * GROUPS.index((dx % X_CHIPS, dy % Y_CHIPS)) + dc % 2


def back_slot(slot):
    dx, dy = GROUPS[slot // 2]
    return slot_of(-dx, -dy, slot % 2)


def fused(
    wins, chunks,
    tile_ref, level_hbm, offset_hbm, qkv_ref, scale_hbm, out_w_ref, shift_tab, scale_tab, gate_tab,
    out_ref,
    level_ref, offset_ref, scale_ref,
    own, beside, tabs, wqkv, wmix, wout, tokens, late_tokens, query, key, value, heads, spread, mine, theirs, ysend,
    local_sem, sent, in_recv, recv_sem, mate_recv, late_recv, head_recv, z_recv, y_recv,
):
    me = lax.axis_index("seq")
    win = lax.axis_index("win")
    segment = lax.axis_index("segment")
    core = lax.rem(me, 2)
    x = lax.rem(me // 2, X_CHIPS)
    y = me // (2 * X_CHIPS)

    def seq_of(slot):
        dx, dy = GROUPS[slot // 2]
        chip = lax.rem(y + dy, Y_CHIPS) * X_CHIPS + lax.rem(x + dx, X_CHIPS)
        return 2 * chip + lax.rem(core + slot % 2, 2)

    def on_seq(slot):
        return {"seq": seq_of(slot)}

    right, left, partner, mate = slot_of(1, 0, 0), slot_of(3, 0, 0), slot_of(0, 1, 0), slot_of(0, 0, 1)
    far, partner_left, partner_right, partner_far = slot_of(2, 0, 0), slot_of(3, 1, 0), slot_of(1, 1, 0), slot_of(2, 1, 0)
    after = {"win": lax.rem(win + 1, wins)}
    before = {"win": lax.rem(win + wins - 1, wins)}
    other = {"segment": 1 - segment}
    across = {"segment": 1 - segment, "seq": seq_of(partner)}

    width = own.shape[1]
    here = own.shape[0]
    half = here // 2
    low = half // 2
    unit = here // PIECES
    per_head = LANES * 3 // 4
    count = spread.shape[1]

    pltpu.make_async_copy(tile_ref, own, local_sem.at[0]).start()
    for i, tab in enumerate((shift_tab, scale_tab, gate_tab)):
        pltpu.make_async_copy(tab, tabs.at[i], local_sem.at[1]).start()
    for i in range(3):
        pltpu.make_async_copy(
            qkv_ref.at[pl.ds(i * per_head, per_head)], wqkv.at[pl.ds(i * LANES, per_head)], local_sem.at[2]
        ).start()
    scalars = [
        pltpu.make_async_copy(src, dst, local_sem.at[3 + i])
        for i, (src, dst) in enumerate(((level_hbm, level_ref), (offset_hbm, offset_ref), (scale_hbm, scale_ref)))
    ]
    for copy in scalars:
        copy.start()

    barrier = pltpu.get_barrier_semaphore()
    greeted = [after, before, across] + [on_seq(s) for s in (right, left, partner, mate)]
    for device in greeted:
        pl.semaphore_signal(barrier, inc=1, device_id=device, device_id_type=MESH)

    for slot in range(count):
        first = pl.multiple_of(seq_of(slot) * per_head, per_head)
        pltpu.make_async_copy(
            out_w_ref.at[pl.ds(first, per_head)], wout.at[pl.ds(slot * per_head, per_head)], local_sem.at[6]
        ).start()
    pltpu.make_async_copy(tile_ref, own, local_sem.at[0]).wait()
    pl.semaphore_wait(barrier, len(greeted))

    def push(src, dst, send, recv, device):
        pltpu.make_async_remote_copy(
            src_ref=src, dst_ref=dst, send_sem=send, recv_sem=recv, device_id=device, device_id_type=MESH
        ).start()

    def arrived(ref, sem):
        pltpu.make_async_remote_copy(
            src_ref=ref, dst_ref=ref, send_sem=sent.at[0], recv_sem=sem, device_id=after, device_id_type=MESH
        ).wait_recv()

    def left_here(ref, sem):
        pltpu.make_async_remote_copy(
            src_ref=ref, dst_ref=ref, send_sem=sem, recv_sem=in_recv.at[0], device_id=after, device_id_type=MESH
        ).wait_send()

    sides = ((0, before), (1, after))
    for h in range(2):
        for s, device in sides:
            part = pl.ds(h * half + s * low, low)
            push(own.at[part], beside.at[part], sent.at[0], in_recv.at[h], device)

    for i in range(3):
        wqkv[pl.ds(i * LANES + per_head, LANES - per_head), :] = jnp.zeros((LANES - per_head, width), wqkv.dtype)
    pltpu.make_async_copy(qkv_ref, wqkv.at[pl.ds(0, 3 * per_head)], local_sem.at[2]).wait()
    wmix[...] = wqkv[...].T
    for copy in scalars:
        copy.wait()
    level = level_ref[0]
    lat_offset = offset_ref[0, 0]
    lon_offset = offset_ref[0, 1]
    pltpu.make_async_copy(tabs, tabs, local_sem.at[1]).wait()
    shift_row = tabs[0, pl.ds(level, 1), :]
    scale_row = tabs[1, pl.ds(level, 1), :]
    gate_row = tabs[2, pl.ds(level, 1), :]
    column = lax.broadcasted_iota(jnp.int32, (half, 1), 0)
    low_end = jnp.where(lon_offset <= low, lon_offset, 0)
    high_start = jnp.where(lon_offset <= low, half, lon_offset)

    def taken(column):
        return jnp.logical_or(column < low_end, column >= high_start)

    late_slots = tuple(range(EARLY, count))
    late_count = len(late_slots) // 2
    late_size = len(late_slots) * unit
    late_order = late_slots[::2] + late_slots[1::2]
    sends = [0]

    def piece(slot, p):
        if slot < EARLY:
            return tokens.at[slot, pl.ds(p * unit, unit)]
        return late_tokens.at[p, late_order.index(slot)]

    def arrival(slot, p):
        if slot >= EARLY:
            return late_recv.at[slot % 2, p]
        return mate_recv.at[slot // 2] if slot % 2 else recv_sem.at[slot // 2, p]

    def send_piece(src_slot, p, device_slot, dst_slot):
        lot = 1 if sends[0] < EARLY * PIECES else 2
        push(piece(src_slot, p), piece(dst_slot, p), sent.at[lot], arrival(dst_slot, p), on_seq(device_slot))
        sends[0] += 1

    for h in range(2):
        part = pl.ds(h * half, half)
        arrived(beside.at[part], in_recv.at[h])
        rows = jnp.where(taken(column), beside[part, :].astype(jnp.float32), own[part, :].astype(jnp.float32))
        centred = rows - jnp.mean(rows, -1, keepdims=True)
        variance = jnp.mean(centred * centred, -1, keepdims=True)
        normed = centred * lax.rsqrt(variance + eps_norm) * scale_row + shift_row
        tokens[0, part, :] = normed.astype(tokens.dtype)
        for p in (2 * h, 2 * h + 1):
            send_piece(0, p, partner, partner)
            send_piece(0, p, right, left)
            send_piece(0, p, left, right)
        for p in (2 * h, 2 * h + 1):
            send_piece(0, p, mate, mate)

    def take(slot, p):
        arrived(piece(slot, p), arrival(slot, p))

    def share(slot, p):
        send_piece(slot, p, mate, slot + 1)

    def project(block, owners, parities, start, places):
        size = block.shape[0]
        each = size // len(owners)
        mixed = jnp.dot(block, wmix[...], preferred_element_type=jnp.float32)
        q = mixed[:, :LANES]
        k = mixed[:, LANES : 2 * LANES]
        v = mixed[:, 2 * LANES :]
        q = q * lax.rsqrt(jnp.sum(q * q, -1, keepdims=True) + eps_norm)
        k = k * lax.rsqrt(jnp.sum(k * k, -1, keepdims=True) + eps_norm)
        lane = lax.broadcasted_iota(jnp.int32, (size, LANES), 1)
        index = lax.broadcasted_iota(jnp.int32, (size, LANES), 0)
        row = jnp.zeros((size, LANES), jnp.int32)
        for i, (slot, parity) in enumerate(zip(owners, parities)):
            row = jnp.where(index >= i * each, 2 * seq_of(slot) + parity, row)
        late = row >= lat_offset
        q = jnp.where(lane == per_head, jnp.where(late, 1.0, 0.0), q)
        q = jnp.where(lane == per_head + 1, jnp.where(late, 0.0, 1.0), q)
        k = jnp.where(lane == per_head, jnp.where(late, 0.0, -far_apart), k)
        k = jnp.where(lane == per_head + 1, jnp.where(late, -far_apart, 0.0), k)
        v = jnp.where(lane == per_head, 1.0, v)
        q = q.astype(query.dtype)
        for first, h, place, extent in places:
            query[h, pl.ds(place, extent), :] = q[first : first + extent]
        at = pl.ds(start, size)
        key[at, :] = k.astype(key.dtype)
        value[at, :] = v.astype(value.dtype)

    def project_groups(g, n):
        for slot in range(2 * g + 1, 2 * (g + n), 2):
            arrived(tokens.at[slot], mate_recv.at[slot // 2])
        block = tokens[pl.ds(2 * g, 2 * n)].reshape(2 * n * here, width)
        slots = range(2 * g, 2 * (g + n))
        project(
            block, [slot for slot in slots for _ in range(2)], (0, 1) * (2 * n), g * 2 * here,
            tuple((i * half, i % 2, (2 * g + i // 2) * half, half) for i in range(4 * n)),
        )

    def project_late(p, n):
        for q in range(p, p + n):
            arrived(late_tokens.at[q, pl.ds(late_count, late_count)], late_recv.at[1, q])
        size = n * late_size
        block = late_tokens[pl.ds(p, n)].reshape(size, width)
        project(
            block, late_order * n, (p // 2,) * (n * len(late_slots)), EARLY * here + p * late_size,
            ((0, p // 2, EARLY * half + p % 2 * late_size, size),),
        )

    take(left, 0)
    send_piece(left, 0, right, far)
    send_piece(left, 0, partner, partner_left)
    share(left, 0)
    take(partner, 0)
    share(partner, 0)
    take(right, 0)
    send_piece(right, 0, partner, partner_right)
    share(right, 0)
    project_groups(0, 1)
    take(right, 1)
    send_piece(right, 1, left, far)
    share(right, 1)
    take(partner, 1)
    send_piece(partner, 1, left, partner_right)
    share(partner, 1)
    take(left, 1)
    share(left, 1)
    take(left, 2)
    send_piece(left, 2, right, far)
    send_piece(partner, 1, right, partner_left)
    share(left, 2)
    take(partner, 2)
    share(partner, 2)
    take(right, 2)
    share(right, 2)
    take(right, 3)
    send_piece(right, 3, left, far)
    share(right, 3)
    send_piece(partner, 2, left, partner_right)
    send_piece(partner, 2, right, partner_left)
    take(partner, 3)
    send_piece(partner, 3, right, partner_left)
    send_piece(partner, 3, left, partner_right)
    share(partner, 3)
    take(left, 3)
    share(left, 3)

    def take_far(p):
        take(far, p)
        send_piece(far, p, partner, partner_far)
        share(far, p)

    def take_late(p):
        mine_here = late_tokens.at[p, pl.ds(0, late_count)]
        arrived(mine_here, late_recv.at[0, p])
        push(mine_here, late_tokens.at[p, pl.ds(late_count, late_count)], sent.at[3], late_recv.at[1, p], on_seq(mate))

    take_far(0)
    project_groups(1, 1)
    take_far(1)
    take_far(2)
    project_groups(2, 2)
    take_far(3)
    take_late(0)
    project_groups(4, 1)
    take_late(1)
    take_late(2)
    take_late(3)
    project_late(0, 2)
    project_late(2, 2)

    factor = scale_ref[0, 0] * math.log2(math.e)

    def scores_of(h, start, size):
        return lax.dot_general(
            query[h, pl.ds(start, size), :], key[...], (((1,), (1,)), ((), ())), preferred_element_type=jnp.float32
        )

    def attend(scores):
        lifted = jnp.exp2((scores - jnp.max(scores, -1, keepdims=True)) * factor)
        mixed = jnp.dot(lifted.astype(jnp.bfloat16), value[...], preferred_element_type=jnp.float32)
        return (mixed / mixed[:, per_head : per_head + 1]).astype(heads.dtype)

    def deliver(slot, h):
        if slot:
            to = back_slot(slot)
            push(heads.at[h, slot], spread.at[h, to], sent.at[4], head_recv.at[h], on_seq(slot))

    middle = count // 2
    blocks = [(h, start) for h in range(2) for start in (middle, 0)]
    upcoming = scores_of(blocks[0][0], blocks[0][1] * half, middle * half)
    for i, (h, start) in enumerate(blocks):
        scores = upcoming
        if i + 1 < len(blocks):
            upcoming = scores_of(blocks[i + 1][0], blocks[i + 1][1] * half, middle * half)
        mixed = attend(scores)
        if start:
            for slot in range(middle, EARLY):
                first = (slot - middle) * half
                heads[h, slot] = mixed[first : first + half]
            for k, slot in enumerate(late_order):
                for p in range(2):
                    first = (EARLY - middle) * half + p * late_size + k * unit
                    heads[h, slot, pl.ds(p * unit, unit), :] = mixed[first : first + unit]
        else:
            heads[h, pl.ds(0, middle)] = mixed.reshape(middle, half, LANES)
            spread[h, 0] = heads[h, 0]
        for slot in reversed(range(start, start + middle)):
            deliver(slot, h)

    span = width // chunks
    pltpu.make_async_copy(out_w_ref, wout, local_sem.at[6]).wait()
    for h in range(2):
        arrived(spread.at[h, pl.ds(1, count - 1)], head_recv.at[h])
        gathered = jnp.concatenate([spread[h, slot][:, :per_head] for slot in range(count)], axis=-1)
        for n in range(chunks):
            attention = jnp.dot(gathered, wout[:, pl.ds(n * span, span)], preferred_element_type=jnp.float32)
            mine[h, n] = attention.astype(mine.dtype)
            for s, device in ((0, after), (1, before)):
                part = pl.ds(s * low, low)
                push(mine.at[h, n, part], theirs.at[h, n, part], sent.at[5], z_recv.at[h, n], device)
    for h in range(2):
        for n in range(chunks):
            rows, columns = pl.ds(h * half, half), pl.ds(n * span, span)
            arrived(theirs.at[h, n], z_recv.at[h, n])
            attention = jnp.where(taken(column), theirs[h, n].astype(jnp.float32), mine[h, n].astype(jnp.float32))
            finished = own[rows, columns].astype(jnp.float32) + gate_row[:, n * span : (n + 1) * span] * attention
            ysend[h, n] = finished.astype(ysend.dtype)
            push(ysend.at[h, n], out_ref.at[rows, columns], sent.at[6], y_recv.at[0], other)
    assert sends[0] == 12 * PIECES
    left_here(own, sent.at[0])
    left_here(tokens, sent.at[1])
    left_here(tokens.at[pl.ds(0, sends[0] // PIECES - EARLY)], sent.at[2])
    left_here(late_tokens.at[:, pl.ds(0, late_count)], sent.at[3])
    left_here(heads.at[:, pl.ds(1, count - 1)], sent.at[4])
    left_here(mine, sent.at[5])
    arrived(out_ref, y_recv.at[0])
    left_here(ysend, sent.at[6])


def shards(
    latents, timesteps, offsets, qkv_weight, logit_scale, out_weight, mod_shift, mod_scale, mod_gate
):
    _, row_count, col_count, width = latents.shape
    wins, seq = lax.axis_size("win"), lax.axis_size("seq")
    here = row_count * col_count
    half = here // 2
    unit = here // PIECES
    steps = mod_shift.shape[1]
    chunks = 3 if width % 384 == 0 else 2
    span = width // chunks
    bf16 = jnp.bfloat16
    in_hbm = pl.BlockSpec(memory_space=pltpu.HBM)
    dma = pltpu.SemaphoreType.DMA
    result = pl.pallas_call(
        functools.partial(fused, wins, chunks),
        out_shape=pltpu.VMEM((here, width), bf16),
        in_specs=[in_hbm] * 9,
        out_specs=pl.BlockSpec(memory_space=pltpu.VMEM),
        scratch_shapes=[
            pltpu.SMEM((1,), jnp.int32),
            pltpu.SMEM((1, 2), jnp.int32),
            pltpu.SMEM((1, 1), jnp.float32),
            pltpu.VMEM((here, width), bf16),
            pltpu.VMEM((here, width), bf16),
            pltpu.VMEM((3, steps, width), jnp.float32),
            pltpu.VMEM((3 * LANES, width), bf16),
            pltpu.VMEM((width, 3 * LANES), bf16),
            pltpu.VMEM((seq * (LANES * 3 // 4), width), bf16),
            pltpu.VMEM((EARLY, here, width), bf16),
            pltpu.VMEM((PIECES, seq - EARLY, unit, width), bf16),
            pltpu.VMEM((2, seq * half, LANES), bf16),
            pltpu.VMEM((seq * here, LANES), bf16),
            pltpu.VMEM((seq * here, LANES), bf16),
            pltpu.VMEM((2, seq, half, LANES), bf16),
            pltpu.VMEM((2, seq, half, LANES), bf16),
            pltpu.VMEM((2, chunks, half, span), bf16),
            pltpu.VMEM((2, chunks, half, span), bf16),
            pltpu.VMEM((2, chunks, half, span), bf16),
            dma((7,)),
            dma((7,)),
            dma((2,)),
            dma((EARLY // 2, PIECES)),
            dma((EARLY // 2,)),
            dma((2, PIECES)),
            dma((2,)),
            dma((2, chunks)),
            dma((1,)),
        ],
        compiler_params=pltpu.CompilerParams(
            collective_id=0, has_side_effects=True, vmem_limit_bytes=56 * 1024 * 1024
        ),
    )(
        latents.reshape(here, width),
        timesteps,
        offsets,
        qkv_weight[0, :, 0, :].T,
        logit_scale,
        out_weight[0],
        mod_shift[0],
        mod_scale[0],
        mod_gate[0],
    )
    return result.reshape(1, row_count, col_count, width)


def solution(mesh):
    in_specs = (
        P("segment", "seq", "win", None),
        P("segment"),
        P("segment", None),
        P("segment", None, "seq", None),
        P("segment", "seq"),
        P("segment", None, None),
        P("segment", None, None),
        P("segment", None, None),
        P("segment", None, None),
    )
    out_specs = P("segment", "seq", "win", None)
    return jax.shard_map(shards, mesh=mesh, in_specs=in_specs, out_specs=out_specs, check_vma=False)
```

time: 59.4 us -> 58.2 us (0.980)
  Pallas kernels: 57.2 us -> 56.1 us
    pallas_call x1, Pallas kernels: 57.2 us -> 56.1 us  [shards(): pl.pallas_call(functools.partial(fused, wins, chunks), out_shape=pltpu.VM...]
where the time goes in v3:
time: 58.2 us; the launch traced here: 58 us
  Pallas kernels  56.1 us (96%)
  between operations  1.3 us (2%)
  local copies, waits for them, and re-layouts  0.68 us (1%)
    pallas_call x1, Pallas kernels, shards(): pl.pallas_call(functools.partial(fused, wins, chunks), out_shape=pltpu.VM...  56.1 us

profile of v3, /device:TPU:1, one launch (start us, length us, event | category | flops | bytes accessed | tf_op | source)
XLA Modules:
  0.0 58.0 jit_solution(3194351021860955578)
XLA Ops:
  1.3 56.1 %shard_map.91 = bf16[64,1536]{1,0:T(8,128)(2,1)S(1)} custom-call(bf16[64,1536]{1,0:T(8,128)(2,1)} %bitcast.12, s32[1]{0:T(128)S(6)} %copy.12.level_hbm, s32[1,2]{1,0:T(1,128)} %offset_hbm.1, bf16[288,1536]{1,0:T(8,128)(2,1)} %bitcast.11, f32[1,1]{1,0:T(1,128)S(6)} %copy.13.scale_hbm, bf16[1536,1536]{1,0:T(8,128)(2,1)} %bitcast.10, f32[32,1536]{1,0:T(8,128)} %bitcast.13, ...), custom_call_target="tpu_custom_call" | custom-call | tf_op jit(solution)/shard_map/pallas_call | solution.py:372
  57.4 0.7 %copy.11 = bf16[1,2,32,1536]{3,2,1,0:T(8,128)(2,1)} copy(bf16[1,2,32,1536]{3,2,1,0:T(8,128)(2,1)S(1)} %bitcast.9) | data formatting | bytes 393216

commit v4 on v3

--- a/solution.py
+++ b/solution.py
@@ -35,7 +35,7 @@
     out_ref,
     level_ref, offset_ref, scale_ref,
     own, beside, tabs, wqkv, wmix, wout, tokens, late_tokens, query, key, value, heads, spread, mine, theirs, ysend,
-    local_sem, sent, in_recv, recv_sem, mate_recv, late_recv, head_recv, z_recv, y_recv,
+    local_sem, sent, in_recv, recv_sem, mate_recv, late_recv, far_recv, head_recv, z_recv, y_recv,
 ):
     me = lax.axis_index("seq")
     win = lax.axis_index("win")
@@ -147,6 +147,10 @@
         return late_tokens.at[p, late_order.index(slot)]
 
     def arrival(slot, p):
+        if (slot, p) == (partner_left, 0):
+            return far_recv.at[PIECES]
+        if slot == partner_far:
+            return far_recv.at[p]
         if slot >= EARLY:
             return late_recv.at[slot % 2, p]
         return mate_recv.at[slot // 2] if slot % 2 else recv_sem.at[slot // 2, p]
@@ -238,13 +242,11 @@
     send_piece(right, 1, left, far)
     share(right, 1)
     take(partner, 1)
-    send_piece(partner, 1, left, partner_right)
     share(partner, 1)
     take(left, 1)
     share(left, 1)
     take(left, 2)
     send_piece(left, 2, right, far)
-    send_piece(partner, 1, right, partner_left)
     share(left, 2)
     take(partner, 2)
     share(partner, 2)
@@ -253,8 +255,9 @@
     take(right, 3)
     send_piece(right, 3, left, far)
     share(right, 3)
-    send_piece(partner, 2, left, partner_right)
-    send_piece(partner, 2, right, partner_left)
+    for p in (1, 2):
+        send_piece(partner, p, left, partner_right)
+        send_piece(partner, p, right, partner_left)
     take(partner, 3)
     send_piece(partner, 3, right, partner_left)
     send_piece(partner, 3, left, partner_right)
@@ -264,25 +267,42 @@
 
     def take_far(p):
         take(far, p)
-        send_piece(far, p, partner, partner_far)
+        if p:
+            send_piece(far, p, partner, partner_far)
         share(far, p)
 
-    def take_late(p):
-        mine_here = late_tokens.at[p, pl.ds(0, late_count)]
-        arrived(mine_here, late_recv.at[0, p])
-        push(mine_here, late_tokens.at[p, pl.ds(late_count, late_count)], sent.at[3], late_recv.at[1, p], on_seq(mate))
+    def pass_on(p, first, n):
+        push(
+            late_tokens.at[p, pl.ds(first, n)], late_tokens.at[p, pl.ds(late_count + first, n)],
+            sent.at[3], late_recv.at[1, p], on_seq(mate),
+        )
+
+    def take_pair(p):
+        here_already = 0 if p else 1
+        arrived(late_tokens.at[p, pl.ds(here_already, 2 - here_already)], late_recv.at[0, p])
+        pass_on(p, 0, 2)
+
+    def take_last(p):
+        take(partner_far, p)
+        pass_on(p, 2, 1)
 
     take_far(0)
+    take(partner_left, 0)
+    send_piece(partner_left, 0, right, partner_far)
+    take_far(1)
     project_groups(1, 1)
-    take_far(1)
     take_far(2)
     project_groups(2, 2)
     take_far(3)
-    take_late(0)
+    take_pair(0)
+    take_pair(1)
     project_groups(4, 1)
-    take_late(1)
-    take_late(2)
-    take_late(3)
+    take_pair(2)
+    take_last(1)
+    take_pair(3)
+    take_last(0)
+    take_last(2)
+    take_last(3)
     project_late(0, 2)
     project_late(2, 2)
 
@@ -400,6 +420,7 @@
             dma((EARLY // 2, PIECES)),
             dma((EARLY // 2,)),
             dma((2, PIECES)),
+            dma((PIECES + 1,)),
             dma((2,)),
             dma((2, chunks)),
             dma((1,)),

time: 58.2 us -> 56.5 us (0.971)
  Pallas kernels: 56.1 us -> 54.4 us
    pallas_call x1, Pallas kernels: 56.1 us -> 54.4 us  [shards(): pl.pallas_call(functools.partial(fused, wins, chunks), out_shape=pltpu.VM...]
where the time goes in v4:
time: 56.5 us; the launch traced here: 56.4 us
  Pallas kernels  54.4 us (96%)
  between operations  1.3 us (2%)
  local copies, waits for them, and re-layouts  0.68 us (1%)
    pallas_call x1, Pallas kernels, shards(): pl.pallas_call(functools.partial(fused, wins, chunks), out_shape=pltpu.VM...  54.4 us

profile of v4, /device:TPU:1, one launch (start us, length us, event | category | flops | bytes accessed | tf_op | source)
XLA Modules:
  0.0 56.4 jit_solution(7586204136776274198)
XLA Ops:
  1.3 54.4 %shard_map.91 = bf16[64,1536]{1,0:T(8,128)(2,1)S(1)} custom-call(bf16[64,1536]{1,0:T(8,128)(2,1)} %bitcast.12, s32[1]{0:T(128)S(6)} %copy.12.level_hbm, s32[1,2]{1,0:T(1,128)} %offset_hbm.1, bf16[288,1536]{1,0:T(8,128)(2,1)} %bitcast.11, f32[1,1]{1,0:T(1,128)S(6)} %copy.13.scale_hbm, bf16[1536,1536]{1,0:T(8,128)(2,1)} %bitcast.10, f32[32,1536]{1,0:T(8,128)} %bitcast.13, ...), custom_call_target="tpu_custom_call" | custom-call | tf_op jit(solution)/shard_map/pallas_call | solution.py:392
  55.7 0.7 %copy.11 = bf16[1,2,32,1536]{3,2,1,0:T(8,128)(2,1)} copy(bf16[1,2,32,1536]{3,2,1,0:T(8,128)(2,1)S(1)} %bitcast.9) | data formatting | bytes 393216

commit v5 on v4

--- a/solution.py
+++ b/solution.py
@@ -137,14 +137,12 @@
 
     late_slots = tuple(range(EARLY, count))
     late_count = len(late_slots) // 2
-    late_size = len(late_slots) * unit
-    late_order = late_slots[::2] + late_slots[1::2]
     sends = [0]
 
     def piece(slot, p):
         if slot < EARLY:
             return tokens.at[slot, pl.ds(p * unit, unit)]
-        return late_tokens.at[p, late_order.index(slot)]
+        return late_tokens.at[slot % 2, p, late_slots.index(slot) // 2]
 
     def arrival(slot, p):
         if (slot, p) == (partner_left, 0):
@@ -152,8 +150,8 @@
         if slot == partner_far:
             return far_recv.at[p]
         if slot >= EARLY:
-            return late_recv.at[slot % 2, p]
-        return mate_recv.at[slot // 2] if slot % 2 else recv_sem.at[slot // 2, p]
+            return late_recv.at[p]
+        return mate_recv.at[slot // 2] if slot % 2 else recv_sem.at[slot // 2 - 1, p]
 
     def send_piece(src_slot, p, device_slot, dst_slot):
         lot = 1 if sends[0] < EARLY * PIECES else 2
@@ -218,14 +216,13 @@
             tuple((i * half, i % 2, (2 * g + i // 2) * half, half) for i in range(4 * n)),
         )
 
-    def project_late(p, n):
-        for q in range(p, p + n):
-            arrived(late_tokens.at[q, pl.ds(late_count, late_count)], late_recv.at[1, q])
-        size = n * late_size
-        block = late_tokens[pl.ds(p, n)].reshape(size, width)
+    def project_late(lane):
+        size = PIECES * late_count * unit
+        pair = size // 2
         project(
-            block, late_order * n, (p // 2,) * (n * len(late_slots)), EARLY * here + p * late_size,
-            ((0, p // 2, EARLY * half + p % 2 * late_size, size),),
+            late_tokens[lane].reshape(size, width), late_slots[lane::2] * PIECES,
+            [p // 2 for p in range(PIECES) for _ in range(late_count)], EARLY * here + lane * size,
+            tuple((h * pair, h, EARLY * half + lane * pair, pair) for h in range(2)),
         )
 
     take(left, 0)
@@ -273,13 +270,13 @@
 
     def pass_on(p, first, n):
         push(
-            late_tokens.at[p, pl.ds(first, n)], late_tokens.at[p, pl.ds(late_count + first, n)],
-            sent.at[3], late_recv.at[1, p], on_seq(mate),
+            late_tokens.at[0, p, pl.ds(first, n)], late_tokens.at[1, p, pl.ds(first, n)],
+            sent.at[3], late_recv.at[PIECES], on_seq(mate),
         )
 
     def take_pair(p):
         here_already = 0 if p else 1
-        arrived(late_tokens.at[p, pl.ds(here_already, 2 - here_already)], late_recv.at[0, p])
+        arrived(late_tokens.at[0, p, pl.ds(here_already, 2 - here_already)], late_recv.at[p])
         pass_on(p, 0, 2)
 
     def take_last(p):
@@ -303,8 +300,9 @@
     take_last(0)
     take_last(2)
     take_last(3)
-    project_late(0, 2)
-    project_late(2, 2)
+    project_late(0)
+    arrived(late_tokens.at[1], late_recv.at[PIECES])
+    project_late(1)
 
     factor = scale_ref[0, 0] * math.log2(math.e)
 
@@ -335,9 +333,9 @@
             for slot in range(middle, EARLY):
                 first = (slot - middle) * half
                 heads[h, slot] = mixed[first : first + half]
-            for k, slot in enumerate(late_order):
+            for slot in late_slots:
                 for p in range(2):
-                    first = (EARLY - middle) * half + p * late_size + k * unit
+                    first = (EARLY - middle) * half + ((slot % 2 * 2 + p) * late_count + (slot - EARLY) // 2) * unit
                     heads[h, slot, pl.ds(p * unit, unit), :] = mixed[first : first + unit]
         else:
             heads[h, pl.ds(0, middle)] = mixed.reshape(middle, half, LANES)
@@ -368,7 +366,7 @@
     left_here(own, sent.at[0])
     left_here(tokens, sent.at[1])
     left_here(tokens.at[pl.ds(0, sends[0] // PIECES - EARLY)], sent.at[2])
-    left_here(late_tokens.at[:, pl.ds(0, late_count)], sent.at[3])
+    left_here(late_tokens.at[0], sent.at[3])
     left_here(heads.at[:, pl.ds(1, count - 1)], sent.at[4])
     left_here(mine, sent.at[5])
     arrived(out_ref, y_recv.at[0])
@@ -405,7 +403,7 @@
             pltpu.VMEM((width, 3 * LANES), bf16),
             pltpu.VMEM((seq * (LANES * 3 // 4), width), bf16),
             pltpu.VMEM((EARLY, here, width), bf16),
-            pltpu.VMEM((PIECES, seq - EARLY, unit, width), bf16),
+            pltpu.VMEM((2, PIECES, (seq - EARLY) // 2, unit, width), bf16),
             pltpu.VMEM((2, seq * half, LANES), bf16),
             pltpu.VMEM((seq * here, LANES), bf16),
             pltpu.VMEM((seq * here, LANES), bf16),
@@ -417,9 +415,9 @@
             dma((7,)),
             dma((7,)),
             dma((2,)),
-            dma((EARLY // 2, PIECES)),
+            dma((EARLY // 2 - 1, PIECES)),
             dma((EARLY // 2,)),
-            dma((2, PIECES)),
+            dma((PIECES + 1,)),
             dma((PIECES + 1,)),
             dma((2,)),
             dma((2, chunks)),

time: 56.5 us -> 56.5 us (level)
  no operation moved by 1% of the time
where the time goes in v5:
time: 56.5 us; the launch traced here: 56.3 us
  Pallas kernels  54.3 us (96%)
  between operations  1.3 us (2%)
  local copies, waits for them, and re-layouts  0.68 us (1%)
    pallas_call x1, Pallas kernels, shards(): pl.pallas_call(functools.partial(fused, wins, chunks), out_shape=pltpu.VM...  54.3 us

profile of v5, /device:TPU:1, one launch (start us, length us, event | category | flops | bytes accessed | tf_op | source)
XLA Modules:
  0.0 56.3 jit_solution(14029911349141847047)
XLA Ops:
  1.3 54.3 %shard_map.91 = bf16[64,1536]{1,0:T(8,128)(2,1)S(1)} custom-call(bf16[64,1536]{1,0:T(8,128)(2,1)} %bitcast.12, s32[1]{0:T(128)S(6)} %copy.12.level_hbm, s32[1,2]{1,0:T(1,128)} %offset_hbm.1, bf16[288,1536]{1,0:T(8,128)(2,1)} %bitcast.11, f32[1,1]{1,0:T(1,128)S(6)} %copy.13.scale_hbm, bf16[1536,1536]{1,0:T(8,128)(2,1)} %bitcast.10, f32[32,1536]{1,0:T(8,128)} %bitcast.13, ...), custom_call_target="tpu_custom_call" | custom-call | tf_op jit(solution)/shard_map/pallas_call | solution.py:390
  55.6 0.7 %copy.11 = bf16[1,2,32,1536]{3,2,1,0:T(8,128)(2,1)} copy(bf16[1,2,32,1536]{3,2,1,0:T(8,128)(2,1)S(1)} %bitcast.9) | data formatting | bytes 393216

commit v6 on v5

--- a/solution.py
+++ b/solution.py
@@ -287,10 +287,10 @@
     take(partner_left, 0)
     send_piece(partner_left, 0, right, partner_far)
     take_far(1)
+    take_far(2)
     project_groups(1, 1)
-    take_far(2)
+    take_far(3)
     project_groups(2, 2)
-    take_far(3)
     take_pair(0)
     take_pair(1)
     project_groups(4, 1)

time: 56.5 us -> 56.4 us (level)
  no operation moved by 1% of the time
where the time goes in v6:
time: 56.4 us; the launch traced here: 56.2 us
  Pallas kernels  54.2 us (96%)
  between operations  1.3 us (2%)
  local copies, waits for them, and re-layouts  0.68 us (1%)
    pallas_call x1, Pallas kernels, shards(): pl.pallas_call(functools.partial(fused, wins, chunks), out_shape=pltpu.VM...  54.2 us

profile of v6, /device:TPU:1, one launch (start us, length us, event | category | flops | bytes accessed | tf_op | source)
XLA Modules:
  0.0 56.2 jit_solution(17345205265216380374)
XLA Ops:
  1.3 54.2 %shard_map.91 = bf16[64,1536]{1,0:T(8,128)(2,1)S(1)} custom-call(bf16[64,1536]{1,0:T(8,128)(2,1)} %bitcast.12, s32[1]{0:T(128)S(6)} %copy.12.level_hbm, s32[1,2]{1,0:T(1,128)} %offset_hbm.1, bf16[288,1536]{1,0:T(8,128)(2,1)} %bitcast.11, f32[1,1]{1,0:T(1,128)S(6)} %copy.13.scale_hbm, bf16[1536,1536]{1,0:T(8,128)(2,1)} %bitcast.10, f32[32,1536]{1,0:T(8,128)} %bitcast.13, ...), custom_call_target="tpu_custom_call" | custom-call | tf_op jit(solution)/shard_map/pallas_call | solution.py:390
  55.5 0.7 %copy.11 = bf16[1,2,32,1536]{3,2,1,0:T(8,128)(2,1)} copy(bf16[1,2,32,1536]{3,2,1,0:T(8,128)(2,1)S(1)} %bitcast.9) | data formatting | bytes 393216
